TPU v7x, 32 devices: a whole 2x2x4 slice. The times are simulated.
32 devices in a mesh: dp: 4 (over x, core), rollout: 8 (over z, y).
Axes of the slice: x: 2, y: 2, z: 4, core: 2. Of those that a mesh axis runs over, the one named last changes fastest.
Arguments:
- queries: bfloat16 [32, 512, 2560], P(('dp', 'rollout')), may hold values from -100 to 100
- resp_keys: bfloat16 [32, 512, 512], P(('dp', 'rollout')), may hold values from -5 to 5
- resp_values: bfloat16 [32, 512, 512], P(('dp', 'rollout')), may hold values from -6 to 6
- prompt_keys: bfloat16 [4, 128, 512], P('dp', 'rollout'), may hold values from -6 to 6
- prompt_values: bfloat16 [4, 128, 512], P('dp', 'rollout'), may hold values from -6 to 6
- d_out: bfloat16 [32, 512, 2560], P(('dp', 'rollout')), may hold values from -6 to 6
- lengths: int32 [32], replicated, may hold values from 64 to 512
- owner: int32 [32], replicated, may hold values from 0 to 3
Outputs:
- attn_out: bfloat16 [32, 512, 2560], P(('dp', 'rollout'))
- d_queries: bfloat16 [32, 512, 2560], P(('dp', 'rollout'))
- d_resp_keys: bfloat16 [32, 512, 512], P(('dp', 'rollout'))
- d_resp_values: bfloat16 [32, 512, 512], P(('dp', 'rollout'))
- d_prompt_keys: float32 [4, 128, 512], P('dp', 'rollout')
- d_prompt_values: float32 [4, 128, 512], P('dp', 'rollout')
Inputs may be any that keep to these rules, and one draw needn't show every extreme that they name: `lengths`: rows of a block at or past its length are padding.
All inputs are finite; a program needn't handle non-finite values.
Results may differ from a plain program's by a relative error of at most 0.0071.
Values may be sent and summed in bfloat16 or wider, within the bound.
A program may use at most 128 MiB of HBM per device.

v0:
```python
import jax
import jax.numpy as jnp
from jax import lax
from jax.sharding import PartitionSpec as P

HEAD_DIM = 128
BLOCK = 512
TILE = 128


def attend(q_rows, d_rows, offset, stride, length, keys, values):
    rows = q_rows.shape[0]
    span = keys.shape[0]
    kv_heads = keys.shape[1] // HEAD_DIM
    group = q_rows.shape[1] // keys.shape[1]
    key_heads = keys.reshape(span, kv_heads, HEAD_DIM)
    val_heads = values.reshape(span, kv_heads, HEAD_DIM)
    key_pos = jnp.arange(span, dtype=jnp.int32) - (span - BLOCK)
    live_rows = jnp.clip((length - offset + stride - 1) // stride, 0, rows)
    turns = (live_rows + TILE - 1) // TILE
    scale = HEAD_DIM ** (-0.5)

    def step(turn, carry):
        out_all, dq_all, dk_sum, dv_sum = carry
        start = (turn * TILE).astype(jnp.int32)
        qt = lax.dynamic_slice_in_dim(q_rows, start, TILE, 0).reshape(
            TILE, kv_heads, group, HEAD_DIM
        )
        dt = lax.dynamic_slice_in_dim(d_rows, start, TILE, 0)
        pos = offset + stride * (start + jnp.arange(TILE, dtype=jnp.int32))
        live = pos < length
        dt = jnp.where(live[:, None], dt, jnp.zeros_like(dt)).reshape(
            TILE, kv_heads, group, HEAD_DIM
        )
        scores = (
            jnp.einsum("tkgd,skd->kgts", qt, key_heads, preferred_element_type=jnp.float32) * scale
        )
        allowed = key_pos[None, :] <= pos[:, None]
        scores = jnp.where(allowed, scores, -1e30)
        top = jnp.max(scores, axis=-1, keepdims=True)
        expd = jnp.exp(scores - top)
        probs = expd / jnp.sum(expd, axis=-1, keepdims=True)
        weights = probs.astype(jnp.bfloat16)
        out = jnp.einsum("kgts,skd->tkgd", weights, val_heads, preferred_element_type=jnp.float32)
        out = out * live.astype(jnp.float32)[:, None, None, None]
        dprob = jnp.einsum("tkgd,skd->kgts", dt, val_heads, preferred_element_type=jnp.float32)
        delta = jnp.einsum("tkgd,tkgd->kgt", dt.astype(jnp.float32), out)
        dscore = (probs * (dprob - delta[..., None]) * scale).astype(jnp.bfloat16)
        dq = jnp.einsum("kgts,skd->tkgd", dscore, key_heads, preferred_element_type=jnp.float32)
        dk_sum = dk_sum + jnp.einsum(
            "kgts,tkgd->skd", dscore, qt, preferred_element_type=jnp.float32
        )
        dv_sum = dv_sum + jnp.einsum(
            "kgts,tkgd->skd", weights, dt, preferred_element_type=jnp.float32
        )
        out_all = lax.dynamic_update_slice_in_dim(
            out_all, out.reshape(TILE, -1).astype(jnp.bfloat16), start, 0
        )
        dq_all = lax.dynamic_update_slice_in_dim(
            dq_all, dq.reshape(TILE, -1).astype(jnp.bfloat16), start, 0
        )
        return (out_all, dq_all, dk_sum, dv_sum)

    init = (
        jnp.zeros((rows, q_rows.shape[1]), jnp.bfloat16),
        jnp.zeros((rows, q_rows.shape[1]), jnp.bfloat16),
        jnp.zeros((span, kv_heads, HEAD_DIM), jnp.float32),
        jnp.zeros((span, kv_heads, HEAD_DIM), jnp.float32),
    )
    out_all, dq_all, dk_sum, dv_sum = lax.fori_loop(jnp.int32(0), turns, step, init)
    return (out_all, dq_all, dk_sum.reshape(span, -1), dv_sum.reshape(span, -1))


def block_inputs(whole_prompt, group_index, keys_block, values_block, width_k):
    prompt_pair = lax.dynamic_index_in_dim(whole_prompt, group_index, 0, keepdims=False)
    keys = jnp.concatenate([prompt_pair[:, :width_k], keys_block], axis=0)
    values = jnp.concatenate([prompt_pair[:, width_k:], values_block], axis=0)
    return (keys, values)


def per_device(queries, resp_keys, resp_values, prompt_keys, prompt_values, d_out, lengths, owner):
    rollout_count = lax.axis_size("rollout")
    groups = lax.axis_size("dp")
    row_base = lax.axis_index("dp") * rollout_count
    here = row_base + lax.axis_index("rollout")
    shard_rows = prompt_keys.shape[1]
    prompt_n = shard_rows * rollout_count
    width_k = prompt_keys.shape[2]
    local_pair = jnp.concatenate([prompt_keys[0], prompt_values[0]], axis=1)
    gathered = lax.all_gather(local_pair, ("dp", "rollout"), axis=0, tiled=True)
    whole_prompt = gathered.reshape(groups, prompt_n, 2 * width_k)
    group_ids = jnp.arange(groups, dtype=jnp.int32)
    own_group = owner[here]
    own_keys, own_values = block_inputs(
        whole_prompt, own_group, resp_keys[0], resp_values[0], width_k
    )
    row_owner = lax.dynamic_slice_in_dim(owner, row_base, rollout_count, 0)
    out, dq, dk_all, dv_all = attend(
        queries[0], d_out[0], 0, 1, lengths[here], own_keys, own_values
    )
    dk_resp = dk_all[prompt_n:]
    dv_resp = dv_all[prompt_n:]
    terms = jnp.concatenate([dk_all[:prompt_n], dv_all[:prompt_n]], axis=1)[None]
    source_groups = row_owner[None]
    pieces = terms.reshape(terms.shape[0], rollout_count, shard_rows, 2 * width_k)
    received = lax.all_to_all(pieces, "rollout", split_axis=1, concat_axis=1, tiled=True)
    picks = (source_groups[:, :, None] == group_ids[None, None, :]).astype(jnp.float32)
    by_group = jnp.einsum("msg,msrc->grc", picks, received, precision=lax.Precision.HIGHEST)
    summed = lax.psum_scatter(by_group, "dp", scatter_dimension=0, tiled=True)[0]
    return (
        out[None],
        dq[None],
        dk_resp.astype(jnp.bfloat16)[None],
        dv_resp.astype(jnp.bfloat16)[None],
        summed[None, :, :width_k],
        summed[None, :, width_k:],
    )


def solution(mesh):
    placed = (
        P(("dp", "rollout"), None, None),
        P(("dp", "rollout"), None, None),
        P(("dp", "rollout"), None, None),
        P("dp", "rollout", None),
        P("dp", "rollout", None),
        P(("dp", "rollout"), None, None),
        P(),
        P(),
    )
    return jax.shard_map(
        per_device,
        mesh=mesh,
        in_specs=placed,
        out_specs=(
            P(("dp", "rollout"), None, None),
            P(("dp", "rollout"), None, None),
            P(("dp", "rollout"), None, None),
            P(("dp", "rollout"), None, None),
            P("dp", "rollout", None),
            P("dp", "rollout", None),
        ),
        check_vma=False,
    )
```

profile of v0, /device:TPU:0, one launch (start us, length us, event | category | flops | bytes accessed | tf_op | source)
XLA Modules:
  0.0 246.8 jit_solution(4386930075554072138)
XLA Ops:
  7.2 1.4 pad_maximum_fusion.2
  8.6 1.2 dynamic_slice.19
  10.5 1.2 dynamic_slice.20
  13.1 1.3 copy.49
  14.3 2.0 copy.50
  16.4 4.5 %copy.47 = bf16[1,512,2560]{1,2,0:T(8,128)(2,1)} copy(bf16[1,512,2560]{2,1,0:T(8,128)(2,1)} %param.10) | data formatting | bytes 5242880 | tf_op args[0]
  20.9 2.6 %copy.51 = bf16[1,512,2560]{1,2,0:T(8,128)(2,1)} copy(bf16[1,512,2560]{2,1,0:T(8,128)(2,1)S(1)} %copy-done.4) | data formatting | bytes 5242880 | tf_op args[5]
  24.2 43.9 %all-gather.2.cloned.1.call-done = bf16[512,1024]{1,0:T(8,128)(2,1)} async-done(((bf16[16,1024]{1,0:T(8,128)(2,1)}), bf16[512,1024]{1,0:T(8,128)(2,1)}) %all-gather.2.cloned.1.call-update) | async-done | bytes 1048592 | tf_op jit(solution)/shard_map/all_gather | solution.py:90
  68.1 1.0 constant_dynamic-slice_fusion.1
  69.3 1.1 pad_maximum_fusion.1
  70.4 1.2 copy.52
  71.6 1.1 broadcast.74.clone
  72.8 1.2 broadcast.74
  74.0 1.7 broadcast.73.clone2
  75.6 1.7 broadcast.73.clone
  77.3 89.0 %while.17 = (s32[]{:T(128)}, bf16[512,2560]{1,0:T(8,128)(2,1)}, bf16[512,2560]{1,0:T(8,128)(2,1)}, f32[640,4,128]{0,2,1:T(8,128)}, f32[640,4,128]{0,2,1:T(8,128)...) while((s32[]{:T(128)}, bf16[512,2560]{1,0:T(8,128)(2,1)}, ...), condition=%wide.region_3.4_spmd.clone, body=%wide.region_0.3_spmd.clone.sunk | while | flops 2540911872 | bytes 83453496 | solution.py:70
  78.1 1.5 dynamic-slice_select_fusion.2
  80.4 1.1 fusion.72
  81.4 3.0 %fusion.73 = (f32[4,5,128]{2,1,0:T(8,128)S(1)}, f32[4,5,128,640]{3,2,1,0:T(8,128)S(1)}) fusion(f32[4,128,5,640]{3,1,2,0:T(8,128)S(1)} %fusion.72, pred[128,640]{1,0:T(8,128)(4,1)S(1)} %broadcast_compare_fusion.4), kind=kOutput, calls=%fused_computation.56.clone.1 | output fusion | flops 9831039 | bytes 13199360 | tf_op jit(solution)/shard_map/while/body/sub | solution.py:41
  85.1 3.1 %fusion.75 = (f32[4,5,128]{2,1,0:T(8,128)S(1)}, bf16[128,4,5,128]{0,3,2,1:T(8,128)(2,1)}) fusion(bf16[4,5,128,128]{2,3,1,0:T(8,128)(2,1)S(1)} %bitcast.151, f32[128]{0:T(128)S(1)} %get-tuple-element.235, bf16[4,5,128,640]{3,2,1,0:T(8,128)(2,1)S(1)} %fusion.74, bf16[640,4,128]{2,0,1:T(8,128)(2,1)} %get-tuple-element.279), kind=kOutput, calls=%fused_computation.23.clone.1 | convolution fusion | flops 421066240 | bytes 5253632 | tf_op jit(solution)/shard_map/while/body/kgts,skd->tkgd/dot_general | solution.py:44
  88.2 3.2 %fusion.78 = f32[640,4,128]{0,2,1:T(8,128)} fusion(f32[640,4,128]{0,2,1:T(8,128)} %get-tuple-element.260, bf16[128,4,5,128]{0,3,2,1:T(8,128)(2,1)S(1)} %bitcast.152, bf16[4,5,128,640]{3,2,1,0:T(8,128)(2,1)S(1)} %fusion.74), kind=kOutput, calls=%fused_computation.20.clone.1 | convolution fusion | flops 419758080 | bytes 6553600 | tf_op jit(solution)/shard_map/while/body/kgts,tkgd->skd/dot_general | solution.py:53
  91.4 3.8 %fusion.76 = bf16[4,5,128,640]{3,2,1,0:T(8,128)(2,1)S(1)} fusion(f32[4,5,128]{2,1,0:T(8,128)S(1)} %get-tuple-element.240, bf16[128,4,5,128]{0,3,2,1:T(8,128)(2,1)S(1)} %bitcast.153, f32[4,5,128,640]{3,2,1,0:T(8,128)S(1)} %get-tuple-element.237, f32[4,5,128]{2,1,0:T(8,128)S(1)} %get-tuple-element.238, bf16[640,4,128]{2,0,1:T(8,128)(2,1)} %get-tuple-element.279), kind=kOutput, calls=%fused_computation.5.clone.1 | convolution fusion | flops 427622400 | bytes 11161600 | tf_op jit(solution)/shard_map/while/body/tkgd,skd->kgts/dot_general | solution.py:46
  95.2 2.2 copy.94
  97.3 3.4 %fusion.77 = f32[640,4,128]{0,2,1:T(8,128)} fusion(f32[640,4,128]{0,2,1:T(8,128)} %get-tuple-element.259, bf16[128,4,5,128]{0,3,2,1:T(8,128)(2,1)} %bitcast.149, bf16[4,5,128,640]{3,2,1,0:T(8,128)(2,1)S(1)} %fusion.76), kind=kOutput, calls=%fused_computation.19.clone.1 | convolution fusion | flops 419758080 | bytes 6553600 | tf_op jit(solution)/shard_map/while/body/kgts,tkgd->skd/dot_general | solution.py:50
  100.7 3.0 %convolution_convert_fusion.2 = bf16[4,5,128,128]{2,3,1,0:T(8,128)(2,1)} fusion(bf16[4,5,128,640]{3,2,1,0:T(8,128)(2,1)S(1)} %fusion.76, bf16[640,4,128]{0,2,1:T(8,128)(2,1)} %copy-done.1), kind=kOutput, calls=%fused_computation.21.clone.1 | convolution fusion | flops 419758080 | bytes 4587520 | tf_op jit(solution)/shard_map/while/body/kgts,skd->tkgd/dot_general | solution.py:49
  103.8 1.4 copy.95
  105.2 0.9 constant_dynamic-update-slice_fusion.5
  106.1 0.9 constant_dynamic-update-slice_fusion.4
  107.8 1.5 dynamic-slice_select_fusion.2
  110.1 1.1 fusion.72
  111.1 3.0 %fusion.73 = (f32[4,5,128]{2,1,0:T(8,128)S(1)}, f32[4,5,128,640]{3,2,1,0:T(8,128)S(1)}) fusion(f32[4,128,5,640]{3,1,2,0:T(8,128)S(1)} %fusion.72, pred[128,640]{1,0:T(8,128)(4,1)S(1)} %broadcast_compare_fusion.4), kind=kOutput, calls=%fused_computation.56.clone.1 | output fusion | flops 9831039 | bytes 13199360 | tf_op jit(solution)/shard_map/while/body/sub | solution.py:41
  114.8 3.1 %fusion.75 = (f32[4,5,128]{2,1,0:T(8,128)S(1)}, bf16[128,4,5,128]{0,3,2,1:T(8,128)(2,1)}) fusion(bf16[4,5,128,128]{2,3,1,0:T(8,128)(2,1)S(1)} %bitcast.151, f32[128]{0:T(128)S(1)} %get-tuple-element.235, bf16[4,5,128,640]{3,2,1,0:T(8,128)(2,1)S(1)} %fusion.74, bf16[640,4,128]{2,0,1:T(8,128)(2,1)} %get-tuple-element.279), kind=kOutput, calls=%fused_computation.23.clone.1 | convolution fusion | flops 421066240 | bytes 5253632 | tf_op jit(solution)/shard_map/while/body/kgts,skd->tkgd/dot_general | solution.py:44
  117.9 3.2 %fusion.78 = f32[640,4,128]{0,2,1:T(8,128)} fusion(f32[640,4,128]{0,2,1:T(8,128)} %get-tuple-element.260, bf16[128,4,5,128]{0,3,2,1:T(8,128)(2,1)S(1)} %bitcast.152, bf16[4,5,128,640]{3,2,1,0:T(8,128)(2,1)S(1)} %fusion.74), kind=kOutput, calls=%fused_computation.20.clone.1 | convolution fusion | flops 419758080 | bytes 6553600 | tf_op jit(solution)/shard_map/while/body/kgts,tkgd->skd/dot_general | solution.py:53
  121.0 3.8 %fusion.76 = bf16[4,5,128,640]{3,2,1,0:T(8,128)(2,1)S(1)} fusion(f32[4,5,128]{2,1,0:T(8,128)S(1)} %get-tuple-element.240, bf16[128,4,5,128]{0,3,2,1:T(8,128)(2,1)S(1)} %bitcast.153, f32[4,5,128,640]{3,2,1,0:T(8,128)S(1)} %get-tuple-element.237, f32[4,5,128]{2,1,0:T(8,128)S(1)} %get-tuple-element.238, bf16[640,4,128]{2,0,1:T(8,128)(2,1)} %get-tuple-element.279), kind=kOutput, calls=%fused_computation.5.clone.1 | convolution fusion | flops 427622400 | bytes 11161600 | tf_op jit(solution)/shard_map/while/body/tkgd,skd->kgts/dot_general | solution.py:46
  124.8 2.2 copy.94
  127.0 3.4 %fusion.77 = f32[640,4,128]{0,2,1:T(8,128)} fusion(f32[640,4,128]{0,2,1:T(8,128)} %get-tuple-element.259, bf16[128,4,5,128]{0,3,2,1:T(8,128)(2,1)} %bitcast.149, bf16[4,5,128,640]{3,2,1,0:T(8,128)(2,1)S(1)} %fusion.76), kind=kOutput, calls=%fused_computation.19.clone.1 | convolution fusion | flops 419758080 | bytes 6553600 | tf_op jit(solution)/shard_map/while/body/kgts,tkgd->skd/dot_general | solution.py:50
  130.4 3.0 %convolution_convert_fusion.2 = bf16[4,5,128,128]{2,3,1,0:T(8,128)(2,1)} fusion(bf16[4,5,128,640]{3,2,1,0:T(8,128)(2,1)S(1)} %fusion.76, bf16[640,4,128]{0,2,1:T(8,128)(2,1)} %copy-done.1), kind=kOutput, calls=%fused_computation.21.clone.1 | convolution fusion | flops 419758080 | bytes 4587520 | tf_op jit(solution)/shard_map/while/body/kgts,skd->tkgd/dot_general | solution.py:49
  133.5 1.4 copy.95
  134.9 0.9 constant_dynamic-update-slice_fusion.5
  135.8 0.9 constant_dynamic-update-slice_fusion.4
  137.5 1.5 dynamic-slice_select_fusion.2
  139.7 1.1 fusion.72
  140.8 3.0 %fusion.73 = (f32[4,5,128]{2,1,0:T(8,128)S(1)}, f32[4,5,128,640]{3,2,1,0:T(8,128)S(1)}) fusion(f32[4,128,5,640]{3,1,2,0:T(8,128)S(1)} %fusion.72, pred[128,640]{1,0:T(8,128)(4,1)S(1)} %broadcast_compare_fusion.4), kind=kOutput, calls=%fused_computation.56.clone.1 | output fusion | flops 9831039 | bytes 13199360 | tf_op jit(solution)/shard_map/while/body/sub | solution.py:41
  144.5 3.1 %fusion.75 = (f32[4,5,128]{2,1,0:T(8,128)S(1)}, bf16[128,4,5,128]{0,3,2,1:T(8,128)(2,1)}) fusion(bf16[4,5,128,128]{2,3,1,0:T(8,128)(2,1)S(1)} %bitcast.151, f32[128]{0:T(128)S(1)} %get-tuple-element.235, bf16[4,5,128,640]{3,2,1,0:T(8,128)(2,1)S(1)} %fusion.74, bf16[640,4,128]{2,0,1:T(8,128)(2,1)} %get-tuple-element.279), kind=kOutput, calls=%fused_computation.23.clone.1 | convolution fusion | flops 421066240 | bytes 5253632 | tf_op jit(solution)/shard_map/while/body/kgts,skd->tkgd/dot_general | solution.py:44
  147.5 3.2 %fusion.78 = f32[640,4,128]{0,2,1:T(8,128)} fusion(f32[640,4,128]{0,2,1:T(8,128)} %get-tuple-element.260, bf16[128,4,5,128]{0,3,2,1:T(8,128)(2,1)S(1)} %bitcast.152, bf16[4,5,128,640]{3,2,1,0:T(8,128)(2,1)S(1)} %fusion.74), kind=kOutput, calls=%fused_computation.20.clone.1 | convolution fusion | flops 419758080 | bytes 6553600 | tf_op jit(solution)/shard_map/while/body/kgts,tkgd->skd/dot_general | solution.py:53
  150.7 3.8 %fusion.76 = bf16[4,5,128,640]{3,2,1,0:T(8,128)(2,1)S(1)} fusion(f32[4,5,128]{2,1,0:T(8,128)S(1)} %get-tuple-element.240, bf16[128,4,5,128]{0,3,2,1:T(8,128)(2,1)S(1)} %bitcast.153, f32[4,5,128,640]{3,2,1,0:T(8,128)S(1)} %get-tuple-element.237, f32[4,5,128]{2,1,0:T(8,128)S(1)} %get-tuple-element.238, bf16[640,4,128]{2,0,1:T(8,128)(2,1)} %get-tuple-element.279), kind=kOutput, calls=%fused_computation.5.clone.1 | convolution fusion | flops 427622400 | bytes 11161600 | tf_op jit(solution)/shard_map/while/body/tkgd,skd->kgts/dot_general | solution.py:46
  154.5 2.2 copy.94
  156.7 3.4 %fusion.77 = f32[640,4,128]{0,2,1:T(8,128)} fusion(f32[640,4,128]{0,2,1:T(8,128)} %get-tuple-element.259, bf16[128,4,5,128]{0,3,2,1:T(8,128)(2,1)} %bitcast.149, bf16[4,5,128,640]{3,2,1,0:T(8,128)(2,1)S(1)} %fusion.76), kind=kOutput, calls=%fused_computation.19.clone.1 | convolution fusion | flops 419758080 | bytes 6553600 | tf_op jit(solution)/shard_map/while/body/kgts,tkgd->skd/dot_general | solution.py:50
  160.1 3.0 %convolution_convert_fusion.2 = bf16[4,5,128,128]{2,3,1,0:T(8,128)(2,1)} fusion(bf16[4,5,128,640]{3,2,1,0:T(8,128)(2,1)S(1)} %fusion.76, bf16[640,4,128]{0,2,1:T(8,128)(2,1)} %copy-done.1), kind=kOutput, calls=%fused_computation.21.clone.1 | convolution fusion | flops 419758080 | bytes 4587520 | tf_op jit(solution)/shard_map/while/body/kgts,skd->tkgd/dot_general | solution.py:49
  163.1 1.4 copy.95
  164.6 0.9 constant_dynamic-update-slice_fusion.5
  165.5 0.9 constant_dynamic-update-slice_fusion.4
  166.3 1.0 slice.35
  167.6 1.0 slice.34
  168.8 0.8 maximum_bitcast_fusion
  169.7 33.1 %all-to-all-start = ((f32[1,8,16,1024]{3,2,0,1:T(8,128)}), f32[1,8,16,1024]{3,2,0,1:T(8,128)S(1)}, u32[]{:S(2)}, u32[]{:S(2)}) async-start(f32[1,8,16,1024]{3,2,0,1:T(8,128)} %maximum_bitcast_fusion), calls=%async_computation | async-start | bytes 1048576 | tf_op jit(solution)/shard_map/all_to_all | solution.py:106
  202.9 16.0 %all-to-all-done = f32[1,8,16,1024]{3,2,0,1:T(8,128)S(1)} async-done(((f32[1,8,16,1024]{3,2,0,1:T(8,128)}), f32[1,8,16,1024]{3,2,0,1:T(8,128)S(1)}, u32[]{:S(2)}, u32[]{:S(2)}) %all-to-all-start) | async-done | bytes 524320 | tf_op jit(solution)/shard_map/all_to_all | solution.py:106
  219.5 0.9 copy.61
  220.4 1.3 slice.48
  221.7 1.3 slice.49
  223.0 1.0 copy.77
  224.0 1.0 copy.76
  225.0 13.5 %reduce-scatter.2.cloned.1.call-done = f32[1,16,1024]{2,1,0:T(8,128)} async-done(((f32[4,16,1024]{2,1,0:T(8,128)}), f32[1,16,1024]{2,1,0:T(8,128)}) %reduce-scatter.2.cloned.1.call-update) | async-done | bytes 65552 | tf_op jit(solution)/shard_map/reduce_scatter | solution.py:109
  238.6 1.4 slice_bitcast_fusion
  (56 shorter events, 8.3 us)
Async XLA Ops:
  7.2 60.9 %all-gather.2.cloned.1.call-start = ((), (), s32[]{:S(2)}) async-start(), calls=%async_computation.2 | async-start | bytes 1081344 | tf_op jit(solution)/shard_map/all_gather | solution.py:90
  16.4 4.5 %copy-start.4 = (bf16[1,512,2560]{2,1,0:T(8,128)(2,1)S(1)}, bf16[1,512,2560]{2,1,0:T(8,128)(2,1)}, u32[]{:S(2)}) copy-start(bf16[1,512,2560]{2,1,0:T(8,128)(2,1)} %param.15) | copy-start | bytes 7864324
  77.3 4.2 %copy-start.1 = (bf16[640,4,128]{0,2,1:T(8,128)(2,1)}, bf16[640,4,128]{0,2,1:T(8,128)(2,1)S(1)}, u32[]{:S(2)}) copy-start(bf16[640,4,128]{0,2,1:T(8,128)(2,1)S(1)} %get-tuple-element.278) | copy-start | bytes 1966084 | tf_op jit(solution)/shard_map/while
  79.5 0.8 copy-start
  103.8 2.3 copy-start.3
  103.8 3.2 %copy-start.2 = (bf16[640,4,128]{0,2,1:T(8,128)(2,1)S(1)}, bf16[640,4,128]{0,2,1:T(8,128)(2,1)}, u32[]{:S(2)}) copy-start(bf16[640,4,128]{0,2,1:T(8,128)(2,1)} %copy-done.1) | copy-start | bytes 1966084 | tf_op jit(solution)/shard_map/while
  107.0 4.2 %copy-start.1 = (bf16[640,4,128]{0,2,1:T(8,128)(2,1)}, bf16[640,4,128]{0,2,1:T(8,128)(2,1)S(1)}, u32[]{:S(2)}) copy-start(bf16[640,4,128]{0,2,1:T(8,128)(2,1)S(1)} %get-tuple-element.278) | copy-start | bytes 1966084 | tf_op jit(solution)/shard_map/while
  109.2 0.8 copy-start
  133.5 2.3 copy-start.3
  133.5 3.2 %copy-start.2 = (bf16[640,4,128]{0,2,1:T(8,128)(2,1)S(1)}, bf16[640,4,128]{0,2,1:T(8,128)(2,1)}, u32[]{:S(2)}) copy-start(bf16[640,4,128]{0,2,1:T(8,128)(2,1)} %copy-done.1) | copy-start | bytes 1966084 | tf_op jit(solution)/shard_map/while
  136.7 4.2 %copy-start.1 = (bf16[640,4,128]{0,2,1:T(8,128)(2,1)}, bf16[640,4,128]{0,2,1:T(8,128)(2,1)S(1)}, u32[]{:S(2)}) copy-start(bf16[640,4,128]{0,2,1:T(8,128)(2,1)S(1)} %get-tuple-element.278) | copy-start | bytes 1966084 | tf_op jit(solution)/shard_map/while
  138.9 0.8 copy-start
  163.1 2.3 copy-start.3
  163.1 3.2 %copy-start.2 = (bf16[640,4,128]{0,2,1:T(8,128)(2,1)S(1)}, bf16[640,4,128]{0,2,1:T(8,128)(2,1)}, u32[]{:S(2)}) copy-start(bf16[640,4,128]{0,2,1:T(8,128)(2,1)} %copy-done.1) | copy-start | bytes 1966084 | tf_op jit(solution)/shard_map/while
  166.3 36.5 %copy-start.5 = (s32[32]{0:T(128)S(1)}, s32[32]{0:T(128)}, u32[]{:S(2)}) copy-start(s32[32]{0:T(128)} %param.17) | copy-start | bytes 388
  169.7 49.2 %all-to-all-start = ((f32[1,8,16,1024]{3,2,0,1:T(8,128)}), f32[1,8,16,1024]{3,2,0,1:T(8,128)S(1)}, u32[]{:S(2)}, u32[]{:S(2)}) async-start(f32[1,8,16,1024]{3,2,0,1:T(8,128)} %maximum_bitcast_fusion), calls=%async_computation | async-start | bytes 1048576 | tf_op jit(solution)/shard_map/all_to_all | solution.py:106
  202.7 35.8 %reduce-scatter.2.cloned.1.call-start = ((), (), s32[]{:S(2)}) async-start(), calls=%async_computation.3 | async-start | bytes 327680 | tf_op jit(solution)/shard_map/reduce_scatter | solution.py:109
Sparse Core Ops, SparseCore 0:
  11.6 56.4 all-gather.1
  220.5 17.9 reduce-scatter.1
where the time goes:
time: 249 us; the launch traced here: 247 us
  waiting for transfers between devices  73.5 us (30%)
  matrix products  53.3 us (21%)
  local copies, waits for them, and re-layouts  48.9 us (20%)
  starting transfers between devices  33.2 us (13%)
  other arithmetic  20.9 us (8%)
  between operations  16.8 us (7%)
    all_gather x1, waiting for transfers between devices, per_device(): gathered = lax.all_gather(local_pair, ('dp', 'rollout'), axis=0, tiled=True)  43.9 us
    all_to_all x1, starting transfers between devices, per_device(): lax.all_to_all(pieces, 'rollout', split_axis=1, concat_axis=1, tiled=True)  33.1 us
    all_to_all x1, waiting for transfers between devices, per_device(): lax.all_to_all(pieces, 'rollout', split_axis=1, concat_axis=1, tiled=True)  16 us
    reduce_scatter x1, waiting for transfers between devices, per_device(): lax.psum_scatter(by_group, 'dp', scatter_dimension=0, tiled=True)[0]  13.5 us
    unnamed x10, local copies, waits for them, and re-layouts  11.8 us
    dot_general x3, matrix products, step(): jnp.einsum('tkgd,skd->kgts', dt, val_heads, preferred_element_type=jnp.fl...  11.4 us
    dot_general x3, matrix products, step(): jnp.einsum('kgts,tkgd->skd', dscore, qt, preferred_element_type=jnp.float32)  10.3 us
    dot_general x3, matrix products, step(): jnp.einsum('kgts,tkgd->skd', weights, dt, preferred_element_type=jnp.floa...  9.58 us
  transfers between devices with their start and end apart: 3, of which 3 were waited for; matrix products, arithmetic and copies ran while one was open for 7% of the time, Pallas kernels for 0%

commit v1 on v0

v1 whole, which is shorter than its diff:
```python
import functools
import math

import jax
import jax.numpy as jnp
from jax import lax
from jax.experimental import pallas as pl
from jax.experimental.pallas import tpu as pltpu
from jax.sharding import PartitionSpec as P

HEAD_DIM = 128
MESH = pl.DeviceIdType.MESH
ROWS = 256
VMEM = pltpu.VMEM


def greet(groups, shards):
    dp, ro = lax.axis_index("dp"), lax.axis_index("rollout")
    barrier = pltpu.get_barrier_semaphore()
    for k in range(1, groups):
        pl.semaphore_signal(
            barrier, inc=1, device_id={"dp": lax.rem(dp + k, groups)}, device_id_type=MESH
        )
    for k in range(1, shards):
        pl.semaphore_signal(
            barrier, inc=1, device_id={"rollout": lax.rem(ro + k, shards)}, device_id_type=MESH
        )
    pl.semaphore_wait(barrier, groups + shards - 2)


def gather_kernel(groups, shards, owner, pk, pv, out, mine, held, stage, s1, r1, s2, r2):
    dp, ro = lax.axis_index("dp"), lax.axis_index("rollout")
    n = mine.shape[1]
    mine[0] = pk[0]
    mine[1] = pv[0]
    greet(groups, shards)
    first = []
    for k in range(1, groups):
        copy = pltpu.make_async_remote_copy(
            src_ref=mine, dst_ref=held.at[k], send_sem=s1.at[k], recv_sem=r1.at[k],
            device_id={"dp": lax.rem(dp + k, groups)}, device_id_type=MESH,
        )
        copy.start()
        first.append(copy)
    held[0] = mine[...]
    for copy in first:
        copy.wait()

    def rows_of(peer):
        return held[lax.rem(dp - owner[dp * shards + peer] + groups, groups)]

    row = pl.ds(pl.multiple_of(ro * n, n), n)
    second = []
    for k in range(1, shards):
        peer = lax.rem(ro + k, shards)
        stage[k] = rows_of(peer)
        copy = pltpu.make_async_remote_copy(
            src_ref=stage.at[k], dst_ref=out.at[:, row, :], send_sem=s2.at[k], recv_sem=r2.at[k],
            device_id={"rollout": peer}, device_id_type=MESH,
        )
        copy.start()
        second.append(copy)
    out[:, row, :] = rows_of(ro)
    for copy in second:
        copy.wait()


def reduce_kernel(groups, shards, owner, term, dpk, dpv, got, acc, stage, got2, s1, r1, s2, r2):
    dp, ro = lax.axis_index("dp"), lax.axis_index("rollout")
    n = got.shape[2]
    greet(groups, shards)
    first = []
    for k in range(1, shards):
        peer = lax.rem(ro + k, shards)
        copy = pltpu.make_async_remote_copy(
            src_ref=term.at[:, pl.ds(pl.multiple_of(peer * n, n), n), :], dst_ref=got.at[k],
            send_sem=s1.at[k], recv_sem=r1.at[k],
            device_id={"rollout": peer}, device_id_type=MESH,
        )
        copy.start()
        first.append(copy)
    got[0] = term[:, pl.ds(pl.multiple_of(ro * n, n), n), :]
    for copy in first:
        copy.wait()
    for k in range(groups):
        target = lax.rem(dp + k, groups)
        total = jnp.zeros(acc.shape, jnp.float32)
        for j in range(shards):
            source = lax.rem(ro - j + shards, shards)
            pick = (owner[dp * shards + source] == target).astype(jnp.float32)
            total = total + pick * got[j].astype(jnp.float32)
        if k == 0:
            acc[...] = total
        else:
            stage[k] = total.astype(jnp.bfloat16)
    second = []
    for k in range(1, groups):
        copy = pltpu.make_async_remote_copy(
            src_ref=stage.at[k], dst_ref=got2.at[k], send_sem=s2.at[k], recv_sem=r2.at[k],
            device_id={"dp": lax.rem(dp + k, groups)}, device_id_type=MESH,
        )
        copy.start()
        second.append(copy)
    for copy in second:
        copy.wait()
    total = acc[...]
    for k in range(1, groups):
        total = total + got2[k].astype(jnp.float32)
    dpk[0] = total[0]
    dpv[0] = total[1]


def dot(a, b, dims=((1,), (0,))):
    return lax.dot_general(a, b, (dims, ((), ())), preferred_element_type=jnp.float32)


def attend_kernel(group, length, q, d, rk, rv, prompt, out, dq, dk, dv, term,
                  kc, vc, kt, vt, dks, dvs):
    block = q.shape[1]
    pn = prompt.shape[1]
    scale = HEAD_DIM ** -0.5
    live_n = length[0]
    kc[:pn] = prompt[0]
    kc[pn:] = rk[0]
    vc[:pn] = prompt[1]
    vc[pn:] = rv[0]
    kt[...] = kc[...].T
    vt[...] = vc[...].T
    dks[...] = jnp.zeros_like(dks)
    dvs[...] = jnp.zeros_like(dvs)
    lead = lax.broadcasted_iota(jnp.int32, (ROWS, ROWS), 0) <= lax.broadcasted_iota(
        jnp.int32, (ROWS, ROWS), 1
    )

    def head(h):
        cols = pl.ds(pl.multiple_of(h * HEAD_DIM, HEAD_DIM), HEAD_DIM)
        for t in range(block // ROWS):
            rows = pl.ds(t * ROWS, ROWS)
            old, span = pn + t * ROWS, pn + (t + 1) * ROWS
            live = (
                lax.broadcasted_iota(jnp.int32, (ROWS, HEAD_DIM), 0) + t * ROWS < live_n
            )
            qt = q[0, rows, cols]
            g = jnp.where(live, d[0, rows, cols].astype(jnp.float32), 0.0).astype(jnp.bfloat16)
            c = scale * math.log2(math.e)
            sa = dot(kc[:old], qt, ((1,), (1,))) * c
            sb = jnp.where(lead, dot(kc[old:span], qt, ((1,), (1,))) * c, -1e30)
            top = jnp.maximum(
                jnp.max(sa, axis=0, keepdims=True), jnp.max(sb, axis=0, keepdims=True)
            )
            ea, eb = jnp.exp2(sa - top), jnp.exp2(sb - top)
            inv = 1.0 / (
                jnp.sum(ea, axis=0, keepdims=True) + jnp.sum(eb, axis=0, keepdims=True)
            )
            p = jnp.concatenate([ea, eb], axis=0) * inv
            w = p.astype(jnp.bfloat16)
            o = dot(vt[:, :span], w)
            out[0, rows, cols] = jnp.where(live, o.T, 0.0).astype(jnp.bfloat16)
            dp = dot(vc[:span], g, ((1,), (1,)))
            delta = jnp.sum(p * dp, axis=0, keepdims=True)
            ds = (p * (dp - delta)).astype(jnp.bfloat16)
            dq[0, rows, cols] = (dot(kt[:, :span], ds) * scale).T.astype(jnp.bfloat16)
            dks[:span] += dot(ds, qt)
            dvs[:span] += dot(w, g)

    for h in range(group):
        head(h)
    dkf = dks[...] * scale
    dk[0] = dkf[pn:].astype(jnp.bfloat16)
    dv[0] = dvs[pn:].astype(jnp.bfloat16)
    term[0] = dkf[:pn].astype(jnp.bfloat16)
    term[1] = dvs[:pn].astype(jnp.bfloat16)


def per_device(queries, resp_keys, resp_values, prompt_keys, prompt_values, d_out, lengths, owner):
    shards = lax.axis_size("rollout")
    groups = lax.axis_size("dp")
    here = lax.axis_index("dp") * shards + lax.axis_index("rollout")
    n, kw = prompt_keys.shape[1:]
    pn = n * shards
    block, qw = queries.shape[1:]
    heads = kw // HEAD_DIM
    group = qw // kw
    span = pn + block
    smem = pl.BlockSpec(memory_space=pltpu.SMEM)
    vmem = pl.BlockSpec(memory_space=pltpu.VMEM)
    dma = pltpu.SemaphoreType.DMA
    bf16, f32 = jnp.bfloat16, jnp.float32

    prompt = pl.pallas_call(
        functools.partial(gather_kernel, groups, shards),
        out_shape=jax.ShapeDtypeStruct((2, pn, kw), bf16),
        in_specs=[smem, vmem, vmem],
        out_specs=vmem,
        scratch_shapes=[
            VMEM((2, n, kw), bf16), VMEM((groups, 2, n, kw), bf16), VMEM((shards, 2, n, kw), bf16),
            dma((groups,)), dma((groups,)), dma((shards,)), dma((shards,)),
        ],
        compiler_params=pltpu.CompilerParams(collective_id=0, has_side_effects=True),
        name="gather_prompt",
    )(owner, prompt_keys, prompt_values)

    wide = pl.BlockSpec((1, block, group * HEAD_DIM), lambda e: (0, 0, e))
    narrow = pl.BlockSpec((1, block, HEAD_DIM), lambda e: (0, 0, e))
    pair = pl.BlockSpec((2, pn, HEAD_DIM), lambda e: (0, 0, e))
    out, dq, dk, dv, term = pl.pallas_call(
        functools.partial(attend_kernel, group),
        grid=(heads,),
        out_shape=(
            jax.ShapeDtypeStruct(queries.shape, bf16),
            jax.ShapeDtypeStruct(queries.shape, bf16),
            jax.ShapeDtypeStruct(resp_keys.shape, bf16),
            jax.ShapeDtypeStruct(resp_keys.shape, bf16),
            jax.ShapeDtypeStruct((2, pn, kw), bf16),
        ),
        in_specs=[smem, wide, wide, narrow, narrow, pair],
        out_specs=(wide, wide, narrow, narrow, pair),
        scratch_shapes=[
            VMEM((span, HEAD_DIM), bf16), VMEM((span, HEAD_DIM), bf16),
            VMEM((HEAD_DIM, span), bf16), VMEM((HEAD_DIM, span), bf16),
            VMEM((span, HEAD_DIM), f32), VMEM((span, HEAD_DIM), f32),
        ],
        compiler_params=pltpu.CompilerParams(
            dimension_semantics=("arbitrary",), vmem_limit_bytes=56 * 1024 * 1024
        ),
        name="attend",
    )(lengths[here][None], queries, d_out, resp_keys, resp_values, prompt)

    shape = jax.ShapeDtypeStruct(prompt_keys.shape, f32)
    dpk, dpv = pl.pallas_call(
        functools.partial(reduce_kernel, groups, shards),
        out_shape=(shape, shape),
        in_specs=[smem, vmem],
        out_specs=(vmem, vmem),
        scratch_shapes=[
            VMEM((shards, 2, n, kw), bf16), VMEM((2, n, kw), f32),
            VMEM((groups, 2, n, kw), bf16), VMEM((groups, 2, n, kw), bf16),
            dma((shards,)), dma((shards,)), dma((groups,)), dma((groups,)),
        ],
        compiler_params=pltpu.CompilerParams(collective_id=1, has_side_effects=True),
        name="reduce_prompt",
    )(owner, term)
    return out, dq, dk, dv, dpk, dpv


def solution(mesh):
    rows = P(("dp", "rollout"), None, None)
    prompt = P("dp", "rollout", None)
    return jax.shard_map(
        per_device,
        mesh=mesh,
        in_specs=(rows, rows, rows, prompt, prompt, rows, P(), P()),
        out_specs=(rows, rows, rows, rows, prompt, prompt),
        check_vma=False,
    )
```

time: 249 us -> 66.6 us (0.27)
  waiting for transfers between devices: 73.5 us -> 0 us
  Pallas kernels: 0 us -> 61.6 us
  matrix products: 53.3 us -> 0 us
  local copies, waits for them, and re-layouts: 48.9 us -> 3.99 us
  starting transfers between devices: 33.2 us -> 0 us
  other arithmetic: 20.9 us -> 0 us
  between operations: 16.8 us -> 0.65 us
    pallas_call x0 -> x3, Pallas kernels: none -> 61.6 us  [the longest x1 30.7 us: per_device(): pl.pallas_call(functools.partial(attend_kernel, group), grid=(heads,), ou...]
    dot_general x19 -> x0, matrix products: 53.3 us -> none  [the longest x3 11.4 us: step(): jnp.einsum('tkgd,skd->kgts', dt, val_heads, preferred_element_type=jnp.fl...]
    all_gather x1 -> x0, waiting for transfers between devices: 43.9 us -> none  [per_device(): gathered = lax.all_gather(local_pair, ('dp', 'rollout'), axis=0, tiled=True)]
    all_to_all x1 -> x0, starting transfers between devices: 33.1 us -> none  [per_device(): lax.all_to_all(pieces, 'rollout', split_axis=1, concat_axis=1, tiled=True)]
    dynamic_update_slice x12 -> x0, local copies, waits for them, and re-layouts: 16.1 us -> none  [the longest x6 9.12 us: step(): lax.dynamic_update_slice_in_dim(out_all, out.reshape(TILE, -1).astype(jnp...]
    all_to_all x1 -> x0, waiting for transfers between devices: 16 us -> none  [per_device(): lax.all_to_all(pieces, 'rollout', split_axis=1, concat_axis=1, tiled=True)]
    reduce_scatter x1 -> x0, waiting for transfers between devices: 13.5 us -> none  [per_device(): lax.psum_scatter(by_group, 'dp', scatter_dimension=0, tiled=True)[0]]
    unnamed x10 -> x2, local copies, waits for them, and re-layouts: 11.8 us -> 2.75 us
  transfers between devices with their start and end apart: 3 -> 0, of which waited for: 3 -> 0; matrix products, arithmetic and copies ran while one was open for 7% -> 0% of each run, Pallas kernels for 0% -> 0%
where the time goes in v1:
time: 66.6 us; the launch traced here: 66.2 us
  Pallas kernels  61.6 us (92%)
  local copies, waits for them, and re-layouts  3.99 us (6%)
    pallas_call x1, Pallas kernels, per_device(): pl.pallas_call(functools.partial(attend_kernel, group), grid=(heads,), ou...  30.7 us
    pallas_call x1, Pallas kernels, per_device(): pl.pallas_call(functools.partial(gather_kernel, groups, shards), out_shap...  16.4 us
    pallas_call x1, Pallas kernels, per_device(): pl.pallas_call(functools.partial(reduce_kernel, groups, shards), out_shap...  14.5 us
    unnamed x2, local copies, waits for them, and re-layouts  2.75 us

profile of v1, /device:TPU:0, one launch (start us, length us, event | category | flops | bytes accessed | tf_op | source)
XLA Modules:
  0.0 66.2 jit_solution(15121004336789075223)
XLA Ops:
  0.6 1.2 %dynamic_slice.3.length = s32[1]{0:T(128)} dynamic-slice(s32[32]{0:T(128)} %param.14, s32[]{:T(128)S(6)} %select_n.3), dynamic_slice_sizes={1} | dynamic-slice | bytes 12 | tf_op jit(solution)/shard_map/dynamic_slice | solution.py:227
  1.9 16.4 %gather_prompt.1.prompt = bf16[2,128,512]{2,1,0:T(8,128)(2,1)} custom-call(s32[32]{0:T(128)} %owner.3, bf16[1,16,512]{2,1,0:T(8,128)(2,1)} %pk.1, bf16[1,16,512]{2,1,0:T(8,128)(2,1)} %pv.1), custom_call_target="tpu_custom_call" | custom-call | tf_op jit(solution)/shard_map/gather_prompt/pallas_call | solution.py:190
  18.3 30.7 %attend.1 = (bf16[1,512,2560]{2,1,0:T(8,128)(2,1)}, bf16[1,512,2560]{2,1,0:T(8,128)(2,1)}, bf16[1,512,512]{2,1,0:T(8,128)(2,1)}, bf16[1,512,512]{2,1,0:T(8,128)(2,1)}, bf16[2,128,512]{2,1,0:T(8,128)(2,1)}) custom-call(s32[1]{0:T(128)} %dynamic_slice.3.length, bf16[1,512,2560]{2,1,0:T(8,128)(2,1)} %q.1, bf16[1,512,2560]{2,1,0:T(8,128)(2,1)} %d.1, ...), custom_call_target="tpu_custom_call" | custom-call | tf_op jit(solution)/shard_map/attend/pallas_call | solution.py:206
  49.0 14.5 %reduce_prompt.1 = (f32[1,16,512]{2,1,0:T(8,128)}, f32[1,16,512]{2,1,0:T(8,128)}) custom-call(s32[32]{0:T(128)} %owner.3, bf16[2,128,512]{2,1,0:T(8,128)(2,1)} %get-tuple-element.17.term), custom_call_target="tpu_custom_call" | custom-call | tf_op jit(solution)/shard_map/reduce_prompt/pallas_call | solution.py:230
  63.5 1.4 %copy.16 = f32[1,16,512]{2,1,0:T(8,128)} copy(f32[1,16,512]{2,1,0:T(8,128)} %get-tuple-element.30) | data formatting | bytes 65536
  64.8 1.4 %copy.17 = f32[1,16,512]{2,1,0:T(8,128)} copy(f32[1,16,512]{2,1,0:T(8,128)} %get-tuple-element.31) | data formatting | bytes 65536
